TPU v7x, 32 devices: a whole 2x2x4 slice. The times are simulated.
32 devices in a mesh: blk: 4 (over z), team: 4 (over y, core), heads: 2 (over x).
Axes of the slice: x: 2, y: 2, z: 4, core: 2. Of those that a mesh axis runs over, the one named last changes fastest.
Arguments:
- queries: bfloat16 [512, 1024], P('blk', ('team', 'heads')), may hold values from -16 to 16
- keys: bfloat16 [512, 256], P(('blk', 'team'), 'heads'), may hold values from -16 to 16
- values: bfloat16 [512, 256], P(('blk', 'team'), 'heads'), may hold values from -6 to 6
- out_grads: bfloat16 [512, 1024], P('blk', ('team', 'heads')), may hold values from -6 to 6
- positions: int32 [512], P('blk'), may hold values from 0 to 511, as said below
Outputs:
- query_grad: bfloat16 [512, 1024], P('blk', ('team', 'heads'))
- key_grad: bfloat16 [512, 256], P(('blk', 'team'), 'heads')
- value_grad: bfloat16 [512, 256], P(('blk', 'team'), 'heads')
Inputs may be any that keep to these rules, and one draw needn't show every extreme that they name: positions hold every number of 0 to 511 once; every aligned run of 32 rows holds 32 consecutive rising positions.
All inputs are finite; a program needn't handle non-finite values.
Results may differ from a plain program's by a relative error of at most 0.0069.
Values may be sent and summed in bfloat16 or wider, within the bound.
A program may use at most 64 MiB of HBM per device.

v0:
```python
import math

import jax
import jax.numpy as jnp
from jax import lax
from jax.sharding import PartitionSpec as P

masked_score = -1e30


def from_behind(block, axis, distance):
    devices = range(lax.axis_size(axis))
    route = [((i - distance) % len(devices), i) for i in devices]
    return lax.ppermute(block, axis, route)


def contract_last(left, right):
    return lax.dot_general(
        left, right, (((1,), (1,)), ((), ())), preferred_element_type=jnp.float32
    )


def contract_first(left, right):
    return lax.dot_general(
        left, right, (((0,), (0,)), ((), ())), preferred_element_type=jnp.float32
    )


def block_terms(data, place_rows, resident):
    query_block, grad_block = data
    keys_all, values_all, key_places = resident
    head_dim = keys_all.shape[1]
    scale = 1.0 / math.sqrt(head_dim)
    row_count = query_block.shape[0]
    scores = contract_last(query_block, keys_all) * scale
    scores = scores.reshape(row_count, -1, keys_all.shape[0])
    visible = place_rows[:, None, None] >= key_places[None, None, :]
    scores = jnp.where(visible, scores, masked_score)
    products = contract_last(grad_block, values_all).reshape(scores.shape)
    return (scores, products, visible)


def rotate_pair(keys_all, values_all):
    return from_behind((keys_all, values_all), "blk", 1)


def per_device(queries, keys, values, out_grads, positions):
    head_dim = keys.shape[1]
    token_rows = queries.shape[0]
    heads_here = queries.shape[1] // head_dim
    scale = 1.0 / math.sqrt(head_dim)
    blocks = lax.axis_size("blk")
    keys_all, values_all = (
        lax.all_gather(keys, "team", axis=0, tiled=True),
        lax.all_gather(values, "team", axis=0, tiled=True),
    )
    places_home = positions.astype(jnp.float32)
    key_count = keys_all.shape[0]
    start_max = jnp.full((token_rows, heads_here), masked_score, jnp.float32)
    start_sum = jnp.zeros((token_rows, heads_here), jnp.float32)
    grad_start = jnp.zeros(queries.shape, jnp.float32)
    kv_start = jnp.zeros((key_count, head_dim), jnp.float32)
    home_data = (queries, out_grads)

    def stat_update(data, places, held, maxima, totals, traces):
        scores, products, visible = block_terms(data, places, held)
        updated = jnp.maximum(maxima, jnp.max(scores, axis=-1))
        weights = jnp.where(visible, jnp.exp(scores - updated[..., None]), 0.0)
        factor = jnp.exp(maxima - updated)
        totals = totals * factor + jnp.sum(weights, axis=-1)
        traces = traces * factor + jnp.sum(weights * products, axis=-1)
        return (updated, totals, traces)

    def grad_update(data, places, held, lse_rows, delta_rows):
        scores, products, visible = block_terms(data, places, held)
        weights = jnp.where(visible, jnp.exp(scores - lse_rows[..., None]), 0.0)
        rounded = weights.astype(jnp.bfloat16).reshape(-1, key_count)
        slopes = (
            (weights * (products - delta_rows[..., None]))
            .astype(jnp.bfloat16)
            .reshape(-1, key_count)
        )
        query_flat = data[0]
        grad_flat = data[1]
        value_part = contract_first(rounded, grad_flat)
        key_part = contract_first(slopes, query_flat) * scale
        query_part = jnp.dot(slopes, held[0], preferred_element_type=jnp.float32) * scale
        return (key_part, value_part, query_part)

    def stat_keys(turn_index, loop_state):
        held_keys, held_values, held_places, maxima, totals, traces = loop_state
        maxima, totals, traces = stat_update(
            home_data, places_home, (held_keys, held_values, held_places), maxima, totals, traces
        )
        held_keys, held_values = rotate_pair(held_keys, held_values)
        held_places = from_behind(held_places, "blk", 1)
        return (held_keys, held_values, held_places, maxima, totals, traces)

    state = lax.fori_loop(
        0, blocks, stat_keys, (keys_all, values_all, places_home, start_max, start_sum, start_sum)
    )
    lse_home = state[3] + jnp.log(state[4])
    delta_home = state[5] / state[4]

    def grad_keys(turn_index, loop_state):
        held_keys, held_values, held_places, key_sum, value_sum, query_sum = loop_state
        key_part, value_part, query_part = grad_update(
            home_data, places_home, (held_keys, held_values, held_places), lse_home, delta_home
        )
        query_sum = query_sum + query_part
        held_keys, held_values = rotate_pair(held_keys, held_values)
        held_places, key_sum, value_sum = from_behind(
            (held_places, key_sum + key_part, value_sum + value_part), "blk", 1
        )
        return (held_keys, held_values, held_places, key_sum, value_sum, query_sum)

    state = lax.fori_loop(
        0, blocks, grad_keys, (keys_all, values_all, places_home, kv_start, kv_start, grad_start)
    )
    key_sum, value_sum, query_total = (state[3], state[4], state[5])
    key_grad, value_grad = (
        lax.psum_scatter(key_sum, "team", scatter_dimension=0, tiled=True),
        lax.psum_scatter(value_sum, "team", scatter_dimension=0, tiled=True),
    )
    return (
        query_total.astype(jnp.bfloat16),
        key_grad.astype(jnp.bfloat16),
        value_grad.astype(jnp.bfloat16),
    )


def solution(mesh):
    in_specs = (
        P("blk", ("team", "heads")),
        P(("blk", "team"), "heads"),
        P(("blk", "team"), "heads"),
        P("blk", ("team", "heads")),
        P("blk"),
    )
    out_specs = (
        P("blk", ("team", "heads")),
        P(("blk", "team"), "heads"),
        P(("blk", "team"), "heads"),
    )
    return jax.shard_map(
        per_device, mesh=mesh, in_specs=in_specs, out_specs=out_specs, check_vma=False
    )
```

profile of v0, /device:TPU:0, one launch (start us, length us, event | category | flops | bytes accessed | tf_op | source)
XLA Modules:
  0.0 147.2 jit_solution(4158563059036579936)
XLA Ops:
  7.2 0.6 copy-done.6
  7.9 6.4 %all_gather.6 = bf16[128,128]{1,0:T(8,128)(2,1)S(1)} all-gather(bf16[32,128]{1,0:T(8,128)(2,1)S(1)} %copy-done.4), channel_id=1, replica_groups=mesh['blk'=4,'team'=4,'heads'=2] {'team'}, dimensions={0}, use_global_device_ids=true | all-gather | bytes 40960 | tf_op jit(solution)/shard_map/all_gather | solution.py:54
  14.3 5.4 %all_gather.7 = bf16[128,128]{1,0:T(8,128)(2,1)S(1)} all-gather(bf16[32,128]{1,0:T(8,128)(2,1)S(1)} %copy-done.5), channel_id=1, replica_groups=mesh['blk'=4,'team'=4,'heads'=2] {'team'}, dimensions={0}, use_global_device_ids=true | all-gather | bytes 40960 | tf_op jit(solution)/shard_map/all_gather | solution.py:55
  19.7 0.7 copy-done
  20.5 30.5 %while.42 = (s32[]{:T(128)}, bf16[128,128]{1,0:T(8,128)(2,1)S(1)}, bf16[128,128]{1,0:T(8,128)(2,1)S(1)}, f32[128]{0:T(128)S(1)}, f32[128,1]{0,1:T(1,128)S(1)}, /...) while((s32[]{:T(128)}, bf16[128,128]{1,0:T(8,128)(2,1)S(1)}, ...), condition=%wide.region_4.5_spmd.clone, body=%wide.region_0.4_spmd.clone.sunk | while | flops 8602499 | bytes 736504 | solution.py:99
  20.5 1.8 %collective-permute-start.2 = (f32[128]{0:T(128)S(1)}, f32[128]{0:T(128)S(1)}, u32[]{:S(2)}, u32[]{:S(2)}) collective-permute-start(f32[128]{0:T(128)S(1)} %copy.18), channel_id=1, source_target_pairs={{24,0},{0,8},{8,16},{16,24},{25,1},{1,9},{9,17},{17,25},{26,2},{2,... | collective-permute-start | bytes 1544 | tf_op jit(solution)/shard_map/while/body/eval_jaxpr/ppermute | solution.py:14
  22.3 1.6 %collective-permute-start = (bf16[128,128]{1,0:T(8,128)(2,1)S(1)}, bf16[128,128]{1,0:T(8,128)(2,1)S(1)}, u32[]{:S(2)}, u32[]{:S(2)}) collective-permute-start(bf16[128,128]{1,0:T(8,128)(2,1)S(1)} %copy.16), channel_id=1, source_target_pairs={{24,0},{0,8},{8,16},{16,24},{25,1},{1,9},{9,17},{17,25},{26,2},{2,... | collective-permute-start | bytes 98312 | tf_op jit(solution)/shard_map/while/body/eval_jaxpr/ppermute | solution.py:14
  23.8 1.6 %collective-permute-start.1 = (bf16[128,128]{1,0:T(8,128)(2,1)S(1)}, bf16[128,128]{1,0:T(8,128)(2,1)S(1)}, u32[]{:S(2)}, u32[]{:S(2)}) collective-permute-start(bf16[128,128]{1,0:T(8,128)(2,1)S(1)} %copy.17), channel_id=1, source_target_pairs={{24,0},{0,8},{8,16},{16,24},{25,1},{1,9},{9,17},{17,25},{26,2},{2,... | collective-permute-start | bytes 98312 | tf_op jit(solution)/shard_map/while/body/eval_jaxpr/ppermute | solution.py:14
  25.9 2.0 %collective-permute-done = bf16[128,128]{1,0:T(8,128)(2,1)S(1)} collective-permute-done((bf16[128,128]{1,0:T(8,128)(2,1)S(1)}, bf16[128,128]{1,0:T(8,128)(2,1)S(1)}, u32[]{:S(2)}, u32[]{:S(2)}) %collective-permute-start) | collective-permute-done | bytes 32800 | tf_op jit(solution)/shard_map/while/body/eval_jaxpr/ppermute | solution.py:14
  28.0 1.6 %collective-permute-done.1 = bf16[128,128]{1,0:T(8,128)(2,1)S(1)} collective-permute-done((bf16[128,128]{1,0:T(8,128)(2,1)S(1)}, bf16[128,128]{1,0:T(8,128)(2,1)S(1)}, u32[]{:S(2)}, u32[]{:S(2)}) %collective-permute-start.1) | collective-permute-done | bytes 32800 | tf_op jit(solution)/shard_map/while/body/eval_jaxpr/ppermute | solution.py:14
  29.7 1.5 collective-permute-start.1
  31.6 3.3 %collective-permute-done.2 = f32[128]{0:T(128)S(1)} collective-permute-done((f32[128]{0:T(128)S(1)}, f32[128]{0:T(128)S(1)}, u32[]{:S(2)}, u32[]{:S(2)}) %collective-permute-start.2) | collective-permute-done | bytes 544 | tf_op jit(solution)/shard_map/while/body/eval_jaxpr/ppermute | solution.py:14
  35.7 0.4 collective-permute-start.2
  36.1 2.4 %collective-permute-start = (bf16[128,128]{1,0:T(8,128)(2,1)S(1)}, bf16[128,128]{1,0:T(8,128)(2,1)S(1)}, u32[]{:S(2)}, u32[]{:S(2)}) collective-permute-start(bf16[128,128]{1,0:T(8,128)(2,1)S(1)} %copy.16), channel_id=1, source_target_pairs={{24,0},{0,8},{8,16},{16,24},{25,1},{1,9},{9,17},{17,25},{26,2},{2,... | collective-permute-start | bytes 98312 | tf_op jit(solution)/shard_map/while/body/eval_jaxpr/ppermute | solution.py:14
  39.3 1.8 %collective-permute-done.2 = f32[128]{0:T(128)S(1)} collective-permute-done((f32[128]{0:T(128)S(1)}, f32[128]{0:T(128)S(1)}, u32[]{:S(2)}, u32[]{:S(2)}) %collective-permute-start.2) | collective-permute-done | bytes 544 | tf_op jit(solution)/shard_map/while/body/eval_jaxpr/ppermute | solution.py:14
  41.0 0.8 collective-permute-done
  41.8 2.8 %collective-permute-done.1 = bf16[128,128]{1,0:T(8,128)(2,1)S(1)} collective-permute-done((bf16[128,128]{1,0:T(8,128)(2,1)S(1)}, bf16[128,128]{1,0:T(8,128)(2,1)S(1)}, u32[]{:S(2)}, u32[]{:S(2)}) %collective-permute-start.1) | collective-permute-done | bytes 32800 | tf_op jit(solution)/shard_map/while/body/eval_jaxpr/ppermute | solution.py:14
  44.7 0.6 collective-permute-start.1
  45.8 4.2 %collective-permute-done.2 = f32[128]{0:T(128)S(1)} collective-permute-done((f32[128]{0:T(128)S(1)}, f32[128]{0:T(128)S(1)}, u32[]{:S(2)}, u32[]{:S(2)}) %collective-permute-start.2) | collective-permute-done | bytes 544 | tf_op jit(solution)/shard_map/while/body/eval_jaxpr/ppermute | solution.py:14
  50.0 0.4 collective-permute-done
  50.4 0.6 collective-permute-done.1
  51.0 47.5 %while.43 = (s32[]{:T(128)}, bf16[128,128]{1,0:T(8,128)(2,1)S(1)}, bf16[128,128]{1,0:T(8,128)(2,1)S(1)}, f32[128]{0:T(128)S(1)}, f32[128,128]{1,0:T(8,128)S(1)},...) while((s32[]{:T(128)}, bf16[128,128]{1,0:T(8,128)(2,1)S(1)}, ...), condition=%wide.region_6.7_spmd.clone, body=%wide.region_5.6_spmd.clone.sunk | while | flops 21217280 | bytes 1840471 | solution.py:117
  51.3 2.4 %collective-permute-start.4 = (bf16[128,128]{1,0:T(8,128)(2,1)S(1)}, bf16[128,128]{1,0:T(8,128)(2,1)S(1)}, u32[]{:S(2)}, u32[]{:S(2)}) collective-permute-start(bf16[128,128]{1,0:T(8,128)(2,1)S(1)} %copy.38), channel_id=1, source_target_pairs={{24,0},{0,8},{8,16},{16,24},{25,1},{1,9},{9,17},{17,25},{26,2},{2,... | collective-permute-start | bytes 98312 | tf_op jit(solution)/shard_map/while/body/eval_jaxpr/ppermute | solution.py:14
  54.5 2.2 %collective-permute-start.6 = (f32[128,128]{1,0:T(8,128)S(1)}, f32[128,128]{1,0:T(8,128)S(1)}, u32[]{:S(2)}, u32[]{:S(2)}) collective-permute-start(f32[128,128]{1,0:T(8,128)S(1)} %fusion.73), channel_id=1, source_target_pairs={{24,0},{0,8},{8,16},{16,24},{25,1},{1,9},{9,17},{17,25},{26,2},{2,... | collective-permute-start | bytes 196616 | tf_op jit(solution)/shard_map/while/body/eval_jaxpr/ppermute | solution.py:14
  57.2 2.5 %collective-permute-done.3 = bf16[128,128]{1,0:T(8,128)(2,1)S(1)} collective-permute-done((bf16[128,128]{1,0:T(8,128)(2,1)S(1)}, bf16[128,128]{1,0:T(8,128)(2,1)S(1)}, u32[]{:S(2)}, u32[]{:S(2)}) %collective-permute-start.3) | collective-permute-done | bytes 32800 | tf_op jit(solution)/shard_map/while/body/eval_jaxpr/ppermute | solution.py:14
  59.7 1.6 %collective-permute-done.6 = f32[128,128]{1,0:T(8,128)S(1)} collective-permute-done((f32[128,128]{1,0:T(8,128)S(1)}, f32[128,128]{1,0:T(8,128)S(1)}, u32[]{:S(2)}, u32[]{:S(2)}) %collective-permute-start.6) | collective-permute-done | bytes 65568 | tf_op jit(solution)/shard_map/while/body/eval_jaxpr/ppermute | solution.py:14
  61.3 1.7 %collective-permute-done.7 = f32[128,128]{1,0:T(8,128)S(1)} collective-permute-done((f32[128,128]{1,0:T(8,128)S(1)}, f32[128,128]{1,0:T(8,128)S(1)}, u32[]{:S(2)}, u32[]{:S(2)}) %collective-permute-start.7) | collective-permute-done | bytes 65568 | tf_op jit(solution)/shard_map/while/body/eval_jaxpr/ppermute | solution.py:14
  63.0 1.2 collective-permute-start.4
  64.2 1.1 collective-permute-start.3
  65.8 2.8 %collective-permute-start.6 = (f32[128,128]{1,0:T(8,128)S(1)}, f32[128,128]{1,0:T(8,128)S(1)}, u32[]{:S(2)}, u32[]{:S(2)}) collective-permute-start(f32[128,128]{1,0:T(8,128)S(1)} %fusion.73), channel_id=1, source_target_pairs={{24,0},{0,8},{8,16},{16,24},{25,1},{1,9},{9,17},{17,25},{26,2},{2,... | collective-permute-start | bytes 196616 | tf_op jit(solution)/shard_map/while/body/eval_jaxpr/ppermute | solution.py:14
  69.0 1.2 collective-permute-done.3
  70.2 1.6 %collective-permute-done.6 = f32[128,128]{1,0:T(8,128)S(1)} collective-permute-done((f32[128,128]{1,0:T(8,128)S(1)}, f32[128,128]{1,0:T(8,128)S(1)}, u32[]{:S(2)}, u32[]{:S(2)}) %collective-permute-start.6) | collective-permute-done | bytes 65568 | tf_op jit(solution)/shard_map/while/body/eval_jaxpr/ppermute | solution.py:14
  71.9 2.9 %collective-permute-done.7 = f32[128,128]{1,0:T(8,128)S(1)} collective-permute-done((f32[128,128]{1,0:T(8,128)S(1)}, f32[128,128]{1,0:T(8,128)S(1)}, u32[]{:S(2)}, u32[]{:S(2)}) %collective-permute-start.7) | collective-permute-done | bytes 65568 | tf_op jit(solution)/shard_map/while/body/eval_jaxpr/ppermute | solution.py:14
  74.9 0.7 collective-permute-start.3
  76.2 4.2 %collective-permute-start.6 = (f32[128,128]{1,0:T(8,128)S(1)}, f32[128,128]{1,0:T(8,128)S(1)}, u32[]{:S(2)}, u32[]{:S(2)}) collective-permute-start(f32[128,128]{1,0:T(8,128)S(1)} %fusion.73), channel_id=1, source_target_pairs={{24,0},{0,8},{8,16},{16,24},{25,1},{1,9},{9,17},{17,25},{26,2},{2,... | collective-permute-start | bytes 196616 | tf_op jit(solution)/shard_map/while/body/eval_jaxpr/ppermute | solution.py:14
  80.9 1.3 collective-permute-done.6
  82.3 4.4 %collective-permute-done.7 = f32[128,128]{1,0:T(8,128)S(1)} collective-permute-done((f32[128,128]{1,0:T(8,128)S(1)}, f32[128,128]{1,0:T(8,128)S(1)}, u32[]{:S(2)}, u32[]{:S(2)}) %collective-permute-start.7) | collective-permute-done | bytes 65568 | tf_op jit(solution)/shard_map/while/body/eval_jaxpr/ppermute | solution.py:14
  86.8 0.7 collective-permute-start.3
  88.0 4.2 %collective-permute-start.6 = (f32[128,128]{1,0:T(8,128)S(1)}, f32[128,128]{1,0:T(8,128)S(1)}, u32[]{:S(2)}, u32[]{:S(2)}) collective-permute-start(f32[128,128]{1,0:T(8,128)S(1)} %fusion.73), channel_id=1, source_target_pairs={{24,0},{0,8},{8,16},{16,24},{25,1},{1,9},{9,17},{17,25},{26,2},{2,... | collective-permute-start | bytes 196616 | tf_op jit(solution)/shard_map/while/body/eval_jaxpr/ppermute | solution.py:14
  92.8 1.3 collective-permute-done.6
  94.1 4.4 %collective-permute-done.7 = f32[128,128]{1,0:T(8,128)S(1)} collective-permute-done((f32[128,128]{1,0:T(8,128)S(1)}, f32[128,128]{1,0:T(8,128)S(1)}, u32[]{:S(2)}, u32[]{:S(2)}) %collective-permute-start.7) | collective-permute-done | bytes 65568 | tf_op jit(solution)/shard_map/while/body/eval_jaxpr/ppermute | solution.py:14
  98.5 0.6 copy-done.3
  99.2 0.7 reduce-scatter.5.cloned.1.call-update
  99.9 0.6 convert_element_type.21
  100.5 16.5 %reduce-scatter.3.cloned.1.call-done = f32[32,128]{1,0:T(8,128)} async-done(((f32[128,128]{1,0:T(8,128)}), f32[32,128]{1,0:T(8,128)}) %reduce-scatter.3.cloned.1.call-update) | async-done | bytes 16400 | tf_op jit(solution)/shard_map/reduce_scatter | solution.py:122
  117.1 1.3 convert_element_type.22
  118.4 20.7 %reduce-scatter.5.cloned.1.call-done = f32[32,128]{1,0:T(8,128)} async-done(((f32[128,128]{1,0:T(8,128)}), f32[32,128]{1,0:T(8,128)}) %reduce-scatter.5.cloned.1.call-update) | async-done | bytes 16400 | tf_op jit(solution)/shard_map/reduce_scatter | solution.py:123
  139.1 1.3 convert_element_type.23
  (123 shorter events, 8.2 us)
Async XLA Ops:
  7.2 109.9 %reduce-scatter.3.cloned.1.call-start = ((), (), s32[]{:S(2)}) async-start(), calls=%async_computation.2 | async-start | bytes 81920 | tf_op jit(solution)/shard_map/reduce_scatter | solution.py:122
  7.2 0.7 copy-start.6
  7.2 0.7 copy-start.4
  7.9 6.4 %copy-start.5 = (bf16[32,128]{1,0:T(8,128)(2,1)S(1)}, bf16[32,128]{1,0:T(8,128)(2,1)}, u32[]{:S(2)}) copy-start(bf16[32,128]{1,0:T(8,128)(2,1)} %param.11) | copy-start | bytes 24580
  19.7 0.8 copy-start
  19.7 0.8 copy-start.1
  20.5 5.4 %collective-permute-start.2 = (f32[128]{0:T(128)S(1)}, f32[128]{0:T(128)S(1)}, u32[]{:S(2)}, u32[]{:S(2)}) collective-permute-start(f32[128]{0:T(128)S(1)} %copy.18), channel_id=1, source_target_pairs={{24,0},{0,8},{8,16},{16,24},{25,1},{1,9},{9,17},{17,25},{26,2},{2,... | collective-permute-start | bytes 1544 | tf_op jit(solution)/shard_map/while/body/eval_jaxpr/ppermute | solution.py:14
  22.3 5.7 %collective-permute-start = (bf16[128,128]{1,0:T(8,128)(2,1)S(1)}, bf16[128,128]{1,0:T(8,128)(2,1)S(1)}, u32[]{:S(2)}, u32[]{:S(2)}) collective-permute-start(bf16[128,128]{1,0:T(8,128)(2,1)S(1)} %copy.16), channel_id=1, source_target_pairs={{24,0},{0,8},{8,16},{16,24},{25,1},{1,9},{9,17},{17,25},{26,2},{2,... | collective-permute-start | bytes 98312 | tf_op jit(solution)/shard_map/while/body/eval_jaxpr/ppermute | solution.py:14
  23.8 5.7 %collective-permute-start.1 = (bf16[128,128]{1,0:T(8,128)(2,1)S(1)}, bf16[128,128]{1,0:T(8,128)(2,1)S(1)}, u32[]{:S(2)}, u32[]{:S(2)}) collective-permute-start(bf16[128,128]{1,0:T(8,128)(2,1)S(1)} %copy.17), channel_id=1, source_target_pairs={{24,0},{0,8},{8,16},{16,24},{25,1},{1,9},{9,17},{17,25},{26,2},{2,... | collective-permute-start | bytes 98312 | tf_op jit(solution)/shard_map/while/body/eval_jaxpr/ppermute | solution.py:14
  29.5 5.4 %collective-permute-start.2 = (f32[128]{0:T(128)S(1)}, f32[128]{0:T(128)S(1)}, u32[]{:S(2)}, u32[]{:S(2)}) collective-permute-start(f32[128]{0:T(128)S(1)} %copy.18), channel_id=1, source_target_pairs={{24,0},{0,8},{8,16},{16,24},{25,1},{1,9},{9,17},{17,25},{26,2},{2,... | collective-permute-start | bytes 1544 | tf_op jit(solution)/shard_map/while/body/eval_jaxpr/ppermute | solution.py:14
  29.6 5.8 %collective-permute-start = (bf16[128,128]{1,0:T(8,128)(2,1)S(1)}, bf16[128,128]{1,0:T(8,128)(2,1)S(1)}, u32[]{:S(2)}, u32[]{:S(2)}) collective-permute-start(bf16[128,128]{1,0:T(8,128)(2,1)S(1)} %copy.16), channel_id=1, source_target_pairs={{24,0},{0,8},{8,16},{16,24},{25,1},{1,9},{9,17},{17,25},{26,2},{2,... | collective-permute-start | bytes 98312 | tf_op jit(solution)/shard_map/while/body/eval_jaxpr/ppermute | solution.py:14
  29.7 6.0 %collective-permute-start.1 = (bf16[128,128]{1,0:T(8,128)(2,1)S(1)}, bf16[128,128]{1,0:T(8,128)(2,1)S(1)}, u32[]{:S(2)}, u32[]{:S(2)}) collective-permute-start(bf16[128,128]{1,0:T(8,128)(2,1)S(1)} %copy.17), channel_id=1, source_target_pairs={{24,0},{0,8},{8,16},{16,24},{25,1},{1,9},{9,17},{17,25},{26,2},{2,... | collective-permute-start | bytes 98312 | tf_op jit(solution)/shard_map/while/body/eval_jaxpr/ppermute | solution.py:14
  35.7 5.4 %collective-permute-start.2 = (f32[128]{0:T(128)S(1)}, f32[128]{0:T(128)S(1)}, u32[]{:S(2)}, u32[]{:S(2)}) collective-permute-start(f32[128]{0:T(128)S(1)} %copy.18), channel_id=1, source_target_pairs={{24,0},{0,8},{8,16},{16,24},{25,1},{1,9},{9,17},{17,25},{26,2},{2,... | collective-permute-start | bytes 1544 | tf_op jit(solution)/shard_map/while/body/eval_jaxpr/ppermute | solution.py:14
  36.1 5.7 %collective-permute-start = (bf16[128,128]{1,0:T(8,128)(2,1)S(1)}, bf16[128,128]{1,0:T(8,128)(2,1)S(1)}, u32[]{:S(2)}, u32[]{:S(2)}) collective-permute-start(bf16[128,128]{1,0:T(8,128)(2,1)S(1)} %copy.16), channel_id=1, source_target_pairs={{24,0},{0,8},{8,16},{16,24},{25,1},{1,9},{9,17},{17,25},{26,2},{2,... | collective-permute-start | bytes 98312 | tf_op jit(solution)/shard_map/while/body/eval_jaxpr/ppermute | solution.py:14
  38.6 6.1 %collective-permute-start.1 = (bf16[128,128]{1,0:T(8,128)(2,1)S(1)}, bf16[128,128]{1,0:T(8,128)(2,1)S(1)}, u32[]{:S(2)}, u32[]{:S(2)}) collective-permute-start(bf16[128,128]{1,0:T(8,128)(2,1)S(1)} %copy.17), channel_id=1, source_target_pairs={{24,0},{0,8},{8,16},{16,24},{25,1},{1,9},{9,17},{17,25},{26,2},{2,... | collective-permute-start | bytes 98312 | tf_op jit(solution)/shard_map/while/body/eval_jaxpr/ppermute | solution.py:14
  44.6 5.4 %collective-permute-start.2 = (f32[128]{0:T(128)S(1)}, f32[128]{0:T(128)S(1)}, u32[]{:S(2)}, u32[]{:S(2)}) collective-permute-start(f32[128]{0:T(128)S(1)} %copy.18), channel_id=1, source_target_pairs={{24,0},{0,8},{8,16},{16,24},{25,1},{1,9},{9,17},{17,25},{26,2},{2,... | collective-permute-start | bytes 1544 | tf_op jit(solution)/shard_map/while/body/eval_jaxpr/ppermute | solution.py:14
  44.6 5.8 %collective-permute-start = (bf16[128,128]{1,0:T(8,128)(2,1)S(1)}, bf16[128,128]{1,0:T(8,128)(2,1)S(1)}, u32[]{:S(2)}, u32[]{:S(2)}) collective-permute-start(bf16[128,128]{1,0:T(8,128)(2,1)S(1)} %copy.16), channel_id=1, source_target_pairs={{24,0},{0,8},{8,16},{16,24},{25,1},{1,9},{9,17},{17,25},{26,2},{2,... | collective-permute-start | bytes 98312 | tf_op jit(solution)/shard_map/while/body/eval_jaxpr/ppermute | solution.py:14
  44.7 6.3 %collective-permute-start.1 = (bf16[128,128]{1,0:T(8,128)(2,1)S(1)}, bf16[128,128]{1,0:T(8,128)(2,1)S(1)}, u32[]{:S(2)}, u32[]{:S(2)}) collective-permute-start(bf16[128,128]{1,0:T(8,128)(2,1)S(1)} %copy.17), channel_id=1, source_target_pairs={{24,0},{0,8},{8,16},{16,24},{25,1},{1,9},{9,17},{17,25},{26,2},{2,... | collective-permute-start | bytes 98312 | tf_op jit(solution)/shard_map/while/body/eval_jaxpr/ppermute | solution.py:14
  51.1 6.2 %collective-permute-start.5 = (f32[128]{0:T(128)S(1)}, f32[128]{0:T(128)S(1)}, u32[]{:S(2)}, u32[]{:S(2)}) collective-permute-start(f32[128]{0:T(128)S(1)} %copy.39), channel_id=1, source_target_pairs={{24,0},{0,8},{8,16},{16,24},{25,1},{1,9},{9,17},{17,25},{26,2},{2,... | collective-permute-start | bytes 1544 | tf_op jit(solution)/shard_map/while/body/eval_jaxpr/ppermute | solution.py:14
  51.3 5.9 %collective-permute-start.4 = (bf16[128,128]{1,0:T(8,128)(2,1)S(1)}, bf16[128,128]{1,0:T(8,128)(2,1)S(1)}, u32[]{:S(2)}, u32[]{:S(2)}) collective-permute-start(bf16[128,128]{1,0:T(8,128)(2,1)S(1)} %copy.38), channel_id=1, source_target_pairs={{24,0},{0,8},{8,16},{16,24},{25,1},{1,9},{9,17},{17,25},{26,2},{2,... | collective-permute-start | bytes 98312 | tf_op jit(solution)/shard_map/while/body/eval_jaxpr/ppermute | solution.py:14
  53.7 6.1 %collective-permute-start.3 = (bf16[128,128]{1,0:T(8,128)(2,1)S(1)}, bf16[128,128]{1,0:T(8,128)(2,1)S(1)}, u32[]{:S(2)}, u32[]{:S(2)}) collective-permute-start(bf16[128,128]{1,0:T(8,128)(2,1)S(1)} %copy.37), channel_id=1, source_target_pairs={{24,0},{0,8},{8,16},{16,24},{25,1},{1,9},{9,17},{17,25},{26,2},{2,... | collective-permute-start | bytes 98312 | tf_op jit(solution)/shard_map/while/body/eval_jaxpr/ppermute | solution.py:14
  54.5 6.8 %collective-permute-start.6 = (f32[128,128]{1,0:T(8,128)S(1)}, f32[128,128]{1,0:T(8,128)S(1)}, u32[]{:S(2)}, u32[]{:S(2)}) collective-permute-start(f32[128,128]{1,0:T(8,128)S(1)} %fusion.73), channel_id=1, source_target_pairs={{24,0},{0,8},{8,16},{16,24},{25,1},{1,9},{9,17},{17,25},{26,2},{2,... | collective-permute-start | bytes 196616 | tf_op jit(solution)/shard_map/while/body/eval_jaxpr/ppermute | solution.py:14
  56.9 6.1 %collective-permute-start.7 = (f32[128,128]{1,0:T(8,128)S(1)}, f32[128,128]{1,0:T(8,128)S(1)}, u32[]{:S(2)}, u32[]{:S(2)}) collective-permute-start(f32[128,128]{1,0:T(8,128)S(1)} %convolution_add_fusion.2), channel_id=1, source_target_pairs={{24,0},{0,8},{8,16},{16,24},{25,1},{1,9},{9,17},{17,25},{26,2},{2,... | collective-permute-start | bytes 196616 | tf_op jit(solution)/shard_map/while/body/eval_jaxpr/ppermute | solution.py:14
  63.0 6.0 %collective-permute-start.5 = (f32[128]{0:T(128)S(1)}, f32[128]{0:T(128)S(1)}, u32[]{:S(2)}, u32[]{:S(2)}) collective-permute-start(f32[128]{0:T(128)S(1)} %copy.39), channel_id=1, source_target_pairs={{24,0},{0,8},{8,16},{16,24},{25,1},{1,9},{9,17},{17,25},{26,2},{2,... | collective-permute-start | bytes 1544 | tf_op jit(solution)/shard_map/while/body/eval_jaxpr/ppermute | solution.py:14
  63.0 6.1 %collective-permute-start.4 = (bf16[128,128]{1,0:T(8,128)(2,1)S(1)}, bf16[128,128]{1,0:T(8,128)(2,1)S(1)}, u32[]{:S(2)}, u32[]{:S(2)}) collective-permute-start(bf16[128,128]{1,0:T(8,128)(2,1)S(1)} %copy.38), channel_id=1, source_target_pairs={{24,0},{0,8},{8,16},{16,24},{25,1},{1,9},{9,17},{17,25},{26,2},{2,... | collective-permute-start | bytes 98312 | tf_op jit(solution)/shard_map/while/body/eval_jaxpr/ppermute | solution.py:14
  64.2 6.1 %collective-permute-start.3 = (bf16[128,128]{1,0:T(8,128)(2,1)S(1)}, bf16[128,128]{1,0:T(8,128)(2,1)S(1)}, u32[]{:S(2)}, u32[]{:S(2)}) collective-permute-start(bf16[128,128]{1,0:T(8,128)(2,1)S(1)} %copy.37), channel_id=1, source_target_pairs={{24,0},{0,8},{8,16},{16,24},{25,1},{1,9},{9,17},{17,25},{26,2},{2,... | collective-permute-start | bytes 98312 | tf_op jit(solution)/shard_map/while/body/eval_jaxpr/ppermute | solution.py:14
  65.8 6.1 %collective-permute-start.6 = (f32[128,128]{1,0:T(8,128)S(1)}, f32[128,128]{1,0:T(8,128)S(1)}, u32[]{:S(2)}, u32[]{:S(2)}) collective-permute-start(f32[128,128]{1,0:T(8,128)S(1)} %fusion.73), channel_id=1, source_target_pairs={{24,0},{0,8},{8,16},{16,24},{25,1},{1,9},{9,17},{17,25},{26,2},{2,... | collective-permute-start | bytes 196616 | tf_op jit(solution)/shard_map/while/body/eval_jaxpr/ppermute | solution.py:14
  68.7 6.1 %collective-permute-start.7 = (f32[128,128]{1,0:T(8,128)S(1)}, f32[128,128]{1,0:T(8,128)S(1)}, u32[]{:S(2)}, u32[]{:S(2)}) collective-permute-start(f32[128,128]{1,0:T(8,128)S(1)} %convolution_add_fusion.2), channel_id=1, source_target_pairs={{24,0},{0,8},{8,16},{16,24},{25,1},{1,9},{9,17},{17,25},{26,2},{2,... | collective-permute-start | bytes 196616 | tf_op jit(solution)/shard_map/while/body/eval_jaxpr/ppermute | solution.py:14
  74.8 6.0 %collective-permute-start.5 = (f32[128]{0:T(128)S(1)}, f32[128]{0:T(128)S(1)}, u32[]{:S(2)}, u32[]{:S(2)}) collective-permute-start(f32[128]{0:T(128)S(1)} %copy.39), channel_id=1, source_target_pairs={{24,0},{0,8},{8,16},{16,24},{25,1},{1,9},{9,17},{17,25},{26,2},{2,... | collective-permute-start | bytes 1544 | tf_op jit(solution)/shard_map/while/body/eval_jaxpr/ppermute | solution.py:14
  74.8 6.0 %collective-permute-start.4 = (bf16[128,128]{1,0:T(8,128)(2,1)S(1)}, bf16[128,128]{1,0:T(8,128)(2,1)S(1)}, u32[]{:S(2)}, u32[]{:S(2)}) collective-permute-start(bf16[128,128]{1,0:T(8,128)(2,1)S(1)} %copy.38), channel_id=1, source_target_pairs={{24,0},{0,8},{8,16},{16,24},{25,1},{1,9},{9,17},{17,25},{26,2},{2,... | collective-permute-start | bytes 98312 | tf_op jit(solution)/shard_map/while/body/eval_jaxpr/ppermute | solution.py:14
  74.9 6.0 %collective-permute-start.3 = (bf16[128,128]{1,0:T(8,128)(2,1)S(1)}, bf16[128,128]{1,0:T(8,128)(2,1)S(1)}, u32[]{:S(2)}, u32[]{:S(2)}) collective-permute-start(bf16[128,128]{1,0:T(8,128)(2,1)S(1)} %copy.37), channel_id=1, source_target_pairs={{24,0},{0,8},{8,16},{16,24},{25,1},{1,9},{9,17},{17,25},{26,2},{2,... | collective-permute-start | bytes 98312 | tf_op jit(solution)/shard_map/while/body/eval_jaxpr/ppermute | solution.py:14
  76.2 6.1 %collective-permute-start.6 = (f32[128,128]{1,0:T(8,128)S(1)}, f32[128,128]{1,0:T(8,128)S(1)}, u32[]{:S(2)}, u32[]{:S(2)}) collective-permute-start(f32[128,128]{1,0:T(8,128)S(1)} %fusion.73), channel_id=1, source_target_pairs={{24,0},{0,8},{8,16},{16,24},{25,1},{1,9},{9,17},{17,25},{26,2},{2,... | collective-permute-start | bytes 196616 | tf_op jit(solution)/shard_map/while/body/eval_jaxpr/ppermute | solution.py:14
  80.5 6.1 %collective-permute-start.7 = (f32[128,128]{1,0:T(8,128)S(1)}, f32[128,128]{1,0:T(8,128)S(1)}, u32[]{:S(2)}, u32[]{:S(2)}) collective-permute-start(f32[128,128]{1,0:T(8,128)S(1)} %convolution_add_fusion.2), channel_id=1, source_target_pairs={{24,0},{0,8},{8,16},{16,24},{25,1},{1,9},{9,17},{17,25},{26,2},{2,... | collective-permute-start | bytes 196616 | tf_op jit(solution)/shard_map/while/body/eval_jaxpr/ppermute | solution.py:14
  86.7 6.0 %collective-permute-start.5 = (f32[128]{0:T(128)S(1)}, f32[128]{0:T(128)S(1)}, u32[]{:S(2)}, u32[]{:S(2)}) collective-permute-start(f32[128]{0:T(128)S(1)} %copy.39), channel_id=1, source_target_pairs={{24,0},{0,8},{8,16},{16,24},{25,1},{1,9},{9,17},{17,25},{26,2},{2,... | collective-permute-start | bytes 1544 | tf_op jit(solution)/shard_map/while/body/eval_jaxpr/ppermute | solution.py:14
  86.7 6.0 %collective-permute-start.4 = (bf16[128,128]{1,0:T(8,128)(2,1)S(1)}, bf16[128,128]{1,0:T(8,128)(2,1)S(1)}, u32[]{:S(2)}, u32[]{:S(2)}) collective-permute-start(bf16[128,128]{1,0:T(8,128)(2,1)S(1)} %copy.38), channel_id=1, source_target_pairs={{24,0},{0,8},{8,16},{16,24},{25,1},{1,9},{9,17},{17,25},{26,2},{2,... | collective-permute-start | bytes 98312 | tf_op jit(solution)/shard_map/while/body/eval_jaxpr/ppermute | solution.py:14
  86.8 6.0 %collective-permute-start.3 = (bf16[128,128]{1,0:T(8,128)(2,1)S(1)}, bf16[128,128]{1,0:T(8,128)(2,1)S(1)}, u32[]{:S(2)}, u32[]{:S(2)}) collective-permute-start(bf16[128,128]{1,0:T(8,128)(2,1)S(1)} %copy.37), channel_id=1, source_target_pairs={{24,0},{0,8},{8,16},{16,24},{25,1},{1,9},{9,17},{17,25},{26,2},{2,... | collective-permute-start | bytes 98312 | tf_op jit(solution)/shard_map/while/body/eval_jaxpr/ppermute | solution.py:14
  88.0 6.1 %collective-permute-start.6 = (f32[128,128]{1,0:T(8,128)S(1)}, f32[128,128]{1,0:T(8,128)S(1)}, u32[]{:S(2)}, u32[]{:S(2)}) collective-permute-start(f32[128,128]{1,0:T(8,128)S(1)} %fusion.73), channel_id=1, source_target_pairs={{24,0},{0,8},{8,16},{16,24},{25,1},{1,9},{9,17},{17,25},{26,2},{2,... | collective-permute-start | bytes 196616 | tf_op jit(solution)/shard_map/while/body/eval_jaxpr/ppermute | solution.py:14
  92.4 6.1 %collective-permute-start.7 = (f32[128,128]{1,0:T(8,128)S(1)}, f32[128,128]{1,0:T(8,128)S(1)}, u32[]{:S(2)}, u32[]{:S(2)}) collective-permute-start(f32[128,128]{1,0:T(8,128)S(1)} %convolution_add_fusion.2), channel_id=1, source_target_pairs={{24,0},{0,8},{8,16},{16,24},{25,1},{1,9},{9,17},{17,25},{26,2},{2,... | collective-permute-start | bytes 196616 | tf_op jit(solution)/shard_map/while/body/eval_jaxpr/ppermute | solution.py:14
  98.5 0.6 copy-start.3
  98.5 0.7 copy-start.2
  99.2 39.9 %reduce-scatter.5.cloned.1.call-start = ((), (), s32[]{:S(2)}) async-start(), calls=%async_computation.3 | async-start | bytes 81920 | tf_op jit(solution)/shard_map/reduce_scatter | solution.py:123
Sparse Core Ops, SparseCore 0:
  99.3 17.7 reduce-scatter.2
  119.5 19.5 reduce-scatter.4
where the time goes:
time: 148 us; the launch traced here: 147 us
  waiting for transfers between devices  79.4 us (54%)
  starting transfers between devices  30.9 us (21%)
  between operations  14.1 us (10%)
  blocking collectives  11.8 us (8%)
  matrix products  4.73 us (3%)
  other arithmetic  3.78 us (3%)
  local copies, waits for them, and re-layouts  2.16 us (1%)
    ppermute x32, waiting for transfers between devices, from_behind(): return lax.ppermute(block, axis, route)  41.5 us
    ppermute x32, starting transfers between devices, from_behind(): return lax.ppermute(block, axis, route)  30.8 us
    reduce_scatter x1, waiting for transfers between devices, per_device(): lax.psum_scatter(value_sum, 'team', scatter_dimension=0, tiled=True)  20.7 us
    reduce_scatter x1, waiting for transfers between devices, per_device(): lax.psum_scatter(key_sum, 'team', scatter_dimension=0, tiled=True)  16.5 us
    all_gather x1, blocking collectives, per_device(): lax.all_gather(keys, 'team', axis=0, tiled=True)  6.36 us
    all_gather x1, blocking collectives, per_device(): lax.all_gather(values, 'team', axis=0, tiled=True)  5.42 us
  transfers between devices with their start and end apart: 34, of which 26 were waited for; matrix products, arithmetic and copies ran while one was open for 5% of the time, Pallas kernels for 0%

commit v1 on v0

v1 whole, which is shorter than its diff:
```python
import functools
import math

import jax
import jax.numpy as jnp
from jax import lax
from jax.experimental import pallas as pl
from jax.experimental.pallas import tpu as pltpu
from jax.sharding import PartitionSpec as P

masked_score = -1e30
MESH = pl.DeviceIdType.MESH


def contract_last(left, right):
    return lax.dot_general(
        left, right, (((1,), (1,)), ((), ())), preferred_element_type=jnp.float32
    )


def contract_first(left, right):
    return lax.dot_general(
        left, right, (((0,), (0,)), ((), ())), preferred_element_type=jnp.float32
    )


def each(count, body):
    if count <= 16:
        for index in range(count):
            body(index)
    else:

        def step(index, carry):
            body(index)
            return carry

        lax.fori_loop(0, count, step, 0)


def join_rows(pieces):
    count, rows, width = pieces.shape
    if rows % 16:
        return pieces.astype(jnp.float32).reshape(count * rows, width).astype(pieces.dtype)
    return pieces.reshape(count * rows, width)


def kernel(
    blocks,
    team,
    q_hbm,
    k_hbm,
    v_hbm,
    g_hbm,
    p_hbm,
    qg_hbm,
    kg_hbm,
    vg_hbm,
    q_ref,
    g_ref,
    p_ref,
    kv,
    places,
    scores,
    products,
    parts,
    landed,
    qg_ref,
    kg_ref,
    vg_ref,
    load_sem,
    kv_send,
    kv_recv,
    place_send,
    place_recv,
    part_send,
    part_recv,
    store_sem,
):
    n = blocks * team
    my_blk, my_team = lax.axis_index("blk"), lax.axis_index("team")
    me = my_blk * team + my_team
    rows, head_dim = q_ref.shape
    piece = k_hbm.shape[0]
    scale = 1.0 / math.sqrt(head_dim)

    def peer_of(index):
        step = index + 1
        blk_now = lax.rem(my_blk + lax.div(jnp.int32(step), jnp.int32(team)), blocks)
        team_now = lax.rem(my_team + lax.rem(jnp.int32(step), jnp.int32(team)), team)
        return blk_now, team_now

    loads = [
        pltpu.make_async_copy(p_hbm, p_ref, load_sem.at[0]),
        pltpu.make_async_copy(k_hbm, kv.at[me, 0], load_sem.at[1]),
        pltpu.make_async_copy(v_hbm, kv.at[me, 1], load_sem.at[2]),
        pltpu.make_async_copy(q_hbm, q_ref, load_sem.at[3]),
        pltpu.make_async_copy(g_hbm, g_ref, load_sem.at[4]),
    ]
    for load in loads:
        load.start()

    barrier = pltpu.get_barrier_semaphore()

    def greet(index):
        blk_now, team_now = peer_of(index)
        pl.semaphore_signal(
            barrier,
            inc=1,
            device_id={"blk": blk_now, "team": team_now},
            device_id_type=MESH,
        )

    each(n - 1, greet)
    loads[0].wait()
    place_row = p_ref[...].astype(jnp.float32)
    places[my_blk] = place_row
    loads[1].wait()
    loads[2].wait()
    pl.semaphore_wait(barrier, n - 1)

    def send_piece(index):
        blk_now, team_now = peer_of(n - 2 - index)
        pltpu.make_async_remote_copy(
            src_ref=kv.at[me],
            dst_ref=kv.at[me],
            send_sem=kv_send,
            recv_sem=kv_recv.at[my_blk],
            device_id={"blk": blk_now, "team": team_now},
            device_id_type=MESH,
        ).start()

    def send_places(index):
        pltpu.make_async_remote_copy(
            src_ref=places.at[my_blk],
            dst_ref=places.at[my_blk],
            send_sem=place_send,
            recv_sem=place_recv,
            device_id={"blk": lax.rem(my_blk + index + 1, blocks)},
            device_id_type=MESH,
        ).start()

    each(blocks - 1, send_places)
    each(n - 1, send_piece)
    loads[3].wait()
    loads[4].wait()
    queries = q_ref[...]
    grads = g_ref[...]

    def wait_bytes(ref, sem):
        pltpu.make_async_copy(ref, ref, sem).wait()

    def block_at(distance):
        return lax.rem(my_blk + distance, blocks)

    def block_keys(blk_now, which):
        return join_rows(kv[pl.ds(blk_now * team, team), which])

    def score_block(distance):
        blk_now = block_at(distance)
        scores[blk_now] = contract_last(block_keys(blk_now, 0), queries) * scale
        products[blk_now] = contract_last(block_keys(blk_now, 1), grads)

    wait_bytes(kv.at[pl.ds(0, team - 1)], kv_recv.at[my_blk])
    score_block(0)

    def far_block(index):
        wait_bytes(kv.at[pl.ds(0, team)], kv_recv.at[block_at(index + 1)])
        score_block(index + 1)

    each(blocks - 1, far_block)
    wait_bytes(places.at[pl.ds(0, blocks - 1)], place_recv)

    def top_of(blk_now, top):
        columns = jnp.transpose(jnp.broadcast_to(places[blk_now], (rows, rows)))
        masked = jnp.where(place_row >= columns, scores[blk_now], masked_score)
        scores[blk_now] = masked
        return jnp.maximum(top, jnp.max(masked, axis=0, keepdims=True))

    def fold(body, init):
        if blocks <= 16:
            for index in range(blocks):
                init = body(index, init)
            return init
        return lax.fori_loop(0, blocks, body, init)

    top = fold(top_of, jnp.full((1, rows), masked_score, jnp.float32))

    def sums_of(blk_now, state):
        total, trace = state
        weights = jnp.exp(scores[blk_now] - top)
        scores[blk_now] = weights
        total = total + jnp.sum(weights, axis=0, keepdims=True)
        trace = trace + jnp.sum(weights * products[blk_now], axis=0, keepdims=True)
        return total, trace

    nought = jnp.zeros((1, rows), jnp.float32)
    total, trace = fold(sums_of, (nought, nought))
    inverse = 1.0 / total
    delta = trace * inverse

    def grad_block(index, query_sum):
        blk_now = block_at(index + 1)
        weights = scores[blk_now] * inverse
        rounded = weights.astype(jnp.bfloat16)
        slopes = (weights * (products[blk_now] - delta)).astype(jnp.bfloat16)
        key_part = jnp.dot(slopes, queries, preferred_element_type=jnp.float32) * scale
        value_part = jnp.dot(rounded, grads, preferred_element_type=jnp.float32)
        group = pl.ds(blk_now * team, team)
        parts[group, 0] = key_part.reshape(team, piece, head_dim).astype(jnp.bfloat16)
        parts[group, 1] = value_part.reshape(team, piece, head_dim).astype(jnp.bfloat16)

        def send_part(team_now):
            pltpu.make_async_remote_copy(
                src_ref=parts.at[blk_now * team + team_now],
                dst_ref=landed.at[me],
                send_sem=part_send,
                recv_sem=part_recv,
                device_id={"blk": blk_now, "team": team_now},
                device_id_type=MESH,
            ).start()

        def send_home(step):
            send_part(lax.rem(my_team + step + 1, team))

        if isinstance(index, int) and index == blocks - 1:
            each(team - 1, send_home)
        else:
            each(team, send_part)
        return query_sum + contract_first(slopes, block_keys(blk_now, 0))

    query_sum = jnp.zeros((rows, head_dim), jnp.float32)
    if blocks <= 16:
        for index in range(blocks):
            query_sum = grad_block(index, query_sum)
    else:
        query_sum = lax.fori_loop(0, blocks - 1, grad_block, query_sum)
        query_sum = grad_block(blocks - 1, query_sum)

    qg_ref[...] = (query_sum * scale).astype(jnp.bfloat16)
    store_query = pltpu.make_async_copy(qg_ref, qg_hbm, store_sem.at[0])
    store_query.start()
    landed[me] = parts[me]
    wait_bytes(kv.at[pl.ds(0, n - 1)], kv_send)
    wait_bytes(places.at[pl.ds(0, blocks - 1)], place_send)
    wait_bytes(landed.at[pl.ds(0, n - 1)], part_recv)
    sums = jnp.sum(landed[...].astype(jnp.float32), axis=0)
    kg_ref[...] = sums[0].astype(jnp.bfloat16)
    vg_ref[...] = sums[1].astype(jnp.bfloat16)
    store_keys = pltpu.make_async_copy(kg_ref, kg_hbm, store_sem.at[1])
    store_values = pltpu.make_async_copy(vg_ref, vg_hbm, store_sem.at[2])
    store_keys.start()
    store_values.start()
    wait_bytes(parts.at[pl.ds(0, n - 1)], part_send)
    store_query.wait()
    store_keys.wait()
    store_values.wait()


def per_device(queries, keys, values, out_grads, positions):
    blocks, team = lax.axis_size("blk"), lax.axis_size("team")
    n = blocks * team
    rows, head_dim = queries.shape
    piece = keys.shape[0]
    any_space = pl.BlockSpec(memory_space=pl.ANY)
    return pl.pallas_call(
        functools.partial(kernel, blocks, team),
        out_shape=(
            jax.ShapeDtypeStruct(queries.shape, jnp.bfloat16),
            jax.ShapeDtypeStruct(keys.shape, jnp.bfloat16),
            jax.ShapeDtypeStruct(values.shape, jnp.bfloat16),
        ),
        in_specs=[any_space] * 5,
        out_specs=(any_space,) * 3,
        scratch_shapes=[
            pltpu.VMEM((rows, head_dim), jnp.bfloat16),
            pltpu.VMEM((rows, head_dim), jnp.bfloat16),
            pltpu.VMEM((1, rows), jnp.int32),
            pltpu.VMEM((n, 2, piece, head_dim), jnp.bfloat16),
            pltpu.VMEM((blocks, 1, rows), jnp.float32),
            pltpu.VMEM((blocks, rows, rows), jnp.float32),
            pltpu.VMEM((blocks, rows, rows), jnp.float32),
            pltpu.VMEM((n, 2, piece, head_dim), jnp.bfloat16),
            pltpu.VMEM((n, 2, piece, head_dim), jnp.bfloat16),
            pltpu.VMEM((rows, head_dim), jnp.bfloat16),
            pltpu.VMEM((piece, head_dim), jnp.bfloat16),
            pltpu.VMEM((piece, head_dim), jnp.bfloat16),
            pltpu.SemaphoreType.DMA((5,)),
            pltpu.SemaphoreType.DMA,
            pltpu.SemaphoreType.DMA((blocks,)),
            pltpu.SemaphoreType.DMA,
            pltpu.SemaphoreType.DMA,
            pltpu.SemaphoreType.DMA,
            pltpu.SemaphoreType.DMA,
            pltpu.SemaphoreType.DMA((3,)),
        ],
        compiler_params=pltpu.CompilerParams(collective_id=0, has_side_effects=True),
    )(queries, keys, values, out_grads, positions.reshape(1, rows))


def solution(mesh):
    in_specs = (
        P("blk", ("team", "heads")),
        P(("blk", "team"), "heads"),
        P(("blk", "team"), "heads"),
        P("blk", ("team", "heads")),
        P("blk"),
    )
    out_specs = (
        P("blk", ("team", "heads")),
        P(("blk", "team"), "heads"),
        P(("blk", "team"), "heads"),
    )
    return jax.shard_map(
        per_device, mesh=mesh, in_specs=in_specs, out_specs=out_specs, check_vma=False
    )
```

time: 148 us -> 23.5 us (0.16)
  waiting for transfers between devices: 79.4 us -> 0 us
  starting transfers between devices: 30.9 us -> 0 us
  Pallas kernels: 0 us -> 19.7 us
  between operations: 14.1 us -> 0.65 us
  blocking collectives: 11.8 us -> 0 us
  matrix products: 4.73 us -> 0 us
  other arithmetic: 3.78 us -> 0 us
    ppermute x32 -> x0, waiting for transfers between devices: 41.5 us -> none  [from_behind(): return lax.ppermute(block, axis, route)]
    reduce_scatter x2 -> x0, waiting for transfers between devices: 37.2 us -> none  [the longest x1 20.7 us: per_device(): lax.psum_scatter(value_sum, 'team', scatter_dimension=0, tiled=True)]
    ppermute x32 -> x0, starting transfers between devices: 30.8 us -> none  [from_behind(): return lax.ppermute(block, axis, route)]
    pallas_call x0 -> x1, Pallas kernels: none -> 19.7 us  [per_device(): pl.pallas_call(functools.partial(kernel, blocks, team), out_shape=(jax.Sh...]
    all_gather x2 -> x0, blocking collectives: 11.8 us -> none  [the longest x1 6.36 us: per_device(): lax.all_gather(keys, 'team', axis=0, tiled=True)]
    dot_general x28 -> x0, matrix products: 4.73 us -> none  [the longest x16 2.69 us: contract_last(): lax.dot_general(left, right, (((1,), (1,)), ((), ())), preferred_element_...]
    convert_element_type x4 -> x0, other arithmetic: 3.26 us -> none  [the longest x1 1.32 us: per_device(): value_grad.astype(jnp.bfloat16)]
  transfers between devices with their start and end apart: 34 -> 0, of which waited for: 26 -> 0; matrix products, arithmetic and copies ran while one was open for 5% -> 0% of each run, Pallas kernels for 0% -> 0%
where the time goes in v1:
time: 23.5 us; the launch traced here: 23.1 us
  Pallas kernels  19.7 us (84%)
  local copies, waits for them, and re-layouts  2.68 us (11%)
  between operations  0.65 us (3%)
    pallas_call x1, Pallas kernels, per_device(): pl.pallas_call(functools.partial(kernel, blocks, team), out_shape=(jax.Sh...  19.7 us
    unnamed x7, local copies, waits for them, and re-layouts  2.68 us

profile of v1, /device:TPU:0, one launch (start us, length us, event | category | flops | bytes accessed | tf_op | source)
XLA Modules:
  0.0 23.1 jit_solution(3415718459327916358)
XLA Ops:
  0.6 19.7 %shard_map.76 = (bf16[128,128]{1,0:T(8,128)(2,1)}, bf16[32,128]{1,0:T(8,128)(2,1)}, bf16[32,128]{1,0:T(8,128)(2,1)}) custom-call(bf16[128,128]{1,0:T(8,128)(2,1)} %q_hbm.1, bf16[32,128]{1,0:T(8,128)(2,1)} %k_hbm.1, bf16[32,128]{1,0:T(8,128)(2,1)} %v_hbm.1, bf16[128,128]{1,0:T(8,128)(2,1)} %g_hbm.1, s32[1,128]{1,0:T(1,128)} %bitcast.1), custom_call_target="tpu_custom_call" | custom-call | tf_op jit(solution)/shard_map/pallas_call | solution.py:265
  20.4 0.0 copy-start.1
  20.4 1.4 %copy.11 = bf16[128,128]{1,0:T(8,128)(2,1)} copy(bf16[128,128]{1,0:T(8,128)(2,1)} %get-tuple-element.6) | data formatting | bytes 65536
  21.8 0.0 copy-done.1
  21.8 0.0 copy-start
  21.8 0.6 %copy.12 = bf16[32,128]{1,0:T(8,128)(2,1)} copy(bf16[32,128]{1,0:T(8,128)(2,1)S(1)} %copy-done.1) | data formatting | bytes 16384
  22.4 0.1 copy-done
  22.5 0.6 %copy.13 = bf16[32,128]{1,0:T(8,128)(2,1)} copy(bf16[32,128]{1,0:T(8,128)(2,1)S(1)} %copy-done) | data formatting | bytes 16384
Async XLA Ops:
  20.4 1.4 %copy-start.1 = (bf16[32,128]{1,0:T(8,128)(2,1)S(1)}, bf16[32,128]{1,0:T(8,128)(2,1)}, u32[]{:S(2)}) copy-start(bf16[32,128]{1,0:T(8,128)(2,1)} %get-tuple-element.7) | copy-start | bytes 24580
  21.8 0.7 %copy-start = (bf16[32,128]{1,0:T(8,128)(2,1)S(1)}, bf16[32,128]{1,0:T(8,128)(2,1)}, u32[]{:S(2)}) copy-start(bf16[32,128]{1,0:T(8,128)(2,1)} %get-tuple-element.8) | copy-start | bytes 24580

commit v2 on v1

v2 whole, which is shorter than its diff:
```python
import functools
import math

import jax
import jax.numpy as jnp
from jax import lax
from jax.experimental import pallas as pl
from jax.experimental.pallas import tpu as pltpu
from jax.sharding import PartitionSpec as P

masked_score = -1e30
MESH = pl.DeviceIdType.MESH


def contract_last(left, right):
    return lax.dot_general(
        left, right, (((1,), (1,)), ((), ())), preferred_element_type=jnp.float32
    )


def contract_first(left, right):
    return lax.dot_general(
        left, right, (((0,), (0,)), ((), ())), preferred_element_type=jnp.float32
    )


def each(count, body):
    if count <= 16:
        for index in range(count):
            body(index)
    else:

        def step(index, carry):
            body(index)
            return carry

        lax.fori_loop(0, count, step, 0)


def join_rows(pieces):
    count, rows, width = pieces.shape
    if rows % 16:
        return pieces.astype(jnp.float32).reshape(count * rows, width).astype(pieces.dtype)
    return pieces.reshape(count * rows, width)


def near_first(index, blocks):
    if index == 0:
        return 0
    return (index + 1) // 2 if index % 2 else blocks - index // 2


def kernel(
    blocks,
    team,
    q_hbm,
    k_hbm,
    v_hbm,
    g_hbm,
    p_hbm,
    qg_ref,
    kg_ref,
    vg_ref,
    q_ref,
    g_ref,
    p_ref,
    kv,
    places,
    scores,
    products,
    slopes_ref,
    parts,
    staged,
    sums_ref,
    landed,
    load_sem,
    own_send,
    own_recv,
    pass_send,
    pass_recv,
    place_send,
    place_recv,
    stage_send,
    stage_recv,
    part_send,
    part_recv,
):
    my_blk, my_team = lax.axis_index("blk"), lax.axis_index("team")
    me = my_blk * team + my_team
    rows, head_dim = q_ref.shape
    piece = k_hbm.shape[0]
    scale = 1.0 / math.sqrt(head_dim)

    def block_at(distance):
        return lax.rem(my_blk + distance, blocks)

    def mate_at(distance):
        return lax.rem(my_team + distance, team)

    def blk_peer(blk_now):
        return {"blk": blk_now, "team": my_team}

    def team_peer(team_now):
        return {"blk": my_blk, "team": team_now}

    def send(src, dst, send_sem, recv_sem, peer):
        pltpu.make_async_remote_copy(
            src_ref=src,
            dst_ref=dst,
            send_sem=send_sem,
            recv_sem=recv_sem,
            device_id=peer,
            device_id_type=MESH,
        ).start()

    def wait_bytes(ref, sem):
        pltpu.make_async_copy(ref, ref, sem).wait()

    loads = [
        pltpu.make_async_copy(p_hbm, p_ref, load_sem.at[0]),
        pltpu.make_async_copy(k_hbm, kv.at[me, 0], load_sem.at[1]),
        pltpu.make_async_copy(v_hbm, kv.at[me, 1], load_sem.at[2]),
        pltpu.make_async_copy(q_hbm, q_ref, load_sem.at[3]),
        pltpu.make_async_copy(g_hbm, g_ref, load_sem.at[4]),
    ]
    for load in loads:
        load.start()

    barrier = pltpu.get_barrier_semaphore()

    def greet(peer):
        pl.semaphore_signal(barrier, inc=1, device_id=peer, device_id_type=MESH)

    each(blocks - 1, lambda i: greet(blk_peer(block_at(i + 1))))
    each(team - 1, lambda i: greet(team_peer(mate_at(i + 1))))
    loads[0].wait()
    place_row = p_ref[...].astype(jnp.float32)
    places[my_blk] = place_row
    loads[1].wait()
    loads[2].wait()
    pl.semaphore_wait(barrier, blocks + team - 2)

    def send_far(index):
        blk_now = block_at(blocks - 1 - index)
        send(kv.at[me], kv.at[me], own_send, own_recv.at[my_blk], blk_peer(blk_now))

    def send_places(index):
        blk_now = block_at(index + 1)
        send(places.at[my_blk], places.at[my_blk], place_send, place_recv, blk_peer(blk_now))

    def pass_on(blk_now):
        slot = kv.at[blk_now * team + my_team]
        each(
            team - 1,
            lambda i: send(slot, slot, pass_send, pass_recv.at[blk_now], team_peer(mate_at(i + 1))),
        )

    each(blocks - 1, send_far)
    pass_on(my_blk)
    each(blocks - 1, send_places)

    def pass_far(distance):
        blk_now = block_at(distance)
        wait_bytes(kv.at[0], own_recv.at[blk_now])
        pass_on(blk_now)

    def block_keys(blk_now, which):
        return join_rows(kv[pl.ds(blk_now * team, team), which])

    def score_block(distance, top):
        blk_now = block_at(distance)
        wait_bytes(kv.at[pl.ds(0, team - 1)], pass_recv.at[blk_now])
        columns = jnp.transpose(jnp.broadcast_to(places[blk_now], (rows, rows)))
        found = contract_last(block_keys(blk_now, 0), queries) * scale
        masked = jnp.where(place_row >= columns, found, masked_score)
        scores[blk_now] = masked
        products[blk_now] = contract_last(block_keys(blk_now, 1), grads)
        return jnp.maximum(top, jnp.max(masked, axis=0, keepdims=True))

    def fold(body, init):
        if blocks <= 16:
            for index in range(blocks):
                init = body(index, init)
            return init
        return lax.fori_loop(0, blocks, body, init)

    loads[3].wait()
    loads[4].wait()
    queries = q_ref[...]
    grads = g_ref[...]
    top = jnp.full((1, rows), masked_score, jnp.float32)
    if blocks <= 16:
        order = [near_first(index, blocks) for index in range(blocks)]
        for distance in order[1:]:
            pass_far(distance)
        wait_bytes(places.at[pl.ds(0, blocks - 1)], place_recv)
        for distance in order:
            top = score_block(distance, top)
    else:
        order = None
        each(blocks - 1, lambda i: pass_far(i + 1))
        wait_bytes(places.at[pl.ds(0, blocks - 1)], place_recv)
        top = fold(score_block, top)

    def sums_of(blk_now, state):
        total, trace = state
        weights = jnp.exp(scores[blk_now] - top)
        scores[blk_now] = weights
        total = total + jnp.sum(weights, axis=0, keepdims=True)
        trace = trace + jnp.sum(weights * products[blk_now], axis=0, keepdims=True)
        return total, trace

    nought = jnp.zeros((1, rows), jnp.float32)
    total, trace = fold(sums_of, (nought, nought))
    inverse = 1.0 / total
    delta = trace * inverse

    def grad_block(distance):
        blk_now = block_at(distance)
        weights = scores[blk_now] * inverse
        rounded = weights.astype(jnp.bfloat16)
        slopes = (weights * (products[blk_now] - delta)).astype(jnp.bfloat16)
        slopes_ref[blk_now] = slopes
        key_part = jnp.dot(slopes, queries, preferred_element_type=jnp.float32) * scale
        value_part = jnp.dot(rounded, grads, preferred_element_type=jnp.float32)
        group = pl.ds(blk_now * team, team)
        parts[group, 0] = key_part.reshape(team, piece, head_dim).astype(jnp.bfloat16)
        parts[group, 1] = value_part.reshape(team, piece, head_dim).astype(jnp.bfloat16)

        def send_part(step):
            team_now = mate_at(step + 1)
            send(
                parts.at[blk_now * team + team_now],
                staged.at[me - my_blk * team + blk_now * team],
                stage_send,
                stage_recv.at[blk_now],
                team_peer(team_now),
            )

        each(team - 1, send_part)

    def team_sum(blk_now):
        wait_bytes(staged.at[pl.ds(0, team - 1)], stage_recv.at[blk_now])
        added = parts[blk_now * team + my_team].astype(jnp.float32)
        for step in range(team - 1):
            added = added + staged[blk_now * team + mate_at(step + 1)].astype(jnp.float32)
        return added

    def send_sum(distance):
        blk_now = block_at(distance)
        sums_ref[blk_now] = team_sum(blk_now).astype(jnp.bfloat16)
        send(sums_ref.at[blk_now], landed.at[my_blk], part_send, part_recv, blk_peer(blk_now))

    def add_query(blk_now, query_sum):
        return query_sum + contract_first(slopes_ref[blk_now], block_keys(blk_now, 0))

    if order:
        for distance in order[::-1]:
            grad_block(distance)
    else:
        each(blocks, lambda i: grad_block(i))
    query_sum = fold(add_query, jnp.zeros((rows, head_dim), jnp.float32))
    qg_ref[...] = (query_sum * scale).astype(jnp.bfloat16)
    if order:
        for distance in order[:0:-1]:
            send_sum(distance)
    else:
        each(blocks - 1, lambda i: send_sum(i + 1))
    sums = team_sum(my_blk)
    wait_bytes(kv.at[pl.ds(0, blocks - 1)], own_send)
    wait_bytes(kv.at[pl.ds(0, blocks * (team - 1))], pass_send)
    wait_bytes(places.at[pl.ds(0, blocks - 1)], place_send)
    wait_bytes(staged.at[pl.ds(0, blocks * (team - 1))], stage_send)
    wait_bytes(landed.at[pl.ds(0, blocks - 1)], part_recv)

    def add_landed(index, sums):
        return sums + landed[block_at(index + 1)].astype(jnp.float32)

    if blocks <= 16:
        for index in range(blocks - 1):
            sums = add_landed(index, sums)
    else:
        sums = lax.fori_loop(0, blocks - 1, add_landed, sums)
    kg_ref[...] = sums[0].astype(jnp.bfloat16)
    vg_ref[...] = sums[1].astype(jnp.bfloat16)
    wait_bytes(sums_ref.at[pl.ds(0, blocks - 1)], part_send)


def put_out(*refs):
    count = (len(refs) - 1) // 2
    copies = [
        pltpu.make_async_copy(refs[i], refs[count + i], refs[-1].at[i]) for i in range(count)
    ]
    for copy in copies:
        copy.start()
    for copy in copies:
        copy.wait()


def per_device(queries, keys, values, out_grads, positions):
    blocks, team = lax.axis_size("blk"), lax.axis_size("team")
    n = blocks * team
    rows, head_dim = queries.shape
    piece = keys.shape[0]
    any_space = pl.BlockSpec(memory_space=pl.ANY)
    near_space = pl.BlockSpec(memory_space=pltpu.VMEM)
    results = (queries, keys, values)
    sends = pltpu.SemaphoreType.DMA
    many = pltpu.SemaphoreType.DMA((blocks,))
    slots = pltpu.VMEM((n, 2, piece, head_dim), jnp.bfloat16)
    few = pltpu.VMEM((blocks, 2, piece, head_dim), jnp.bfloat16)
    square = pltpu.VMEM((blocks, rows, rows), jnp.float32)
    held = pl.pallas_call(
        functools.partial(kernel, blocks, team),
        out_shape=tuple(pltpu.VMEM(one.shape, jnp.bfloat16) for one in results),
        in_specs=[any_space] * 5,
        out_specs=(near_space,) * 3,
        scratch_shapes=[
            pltpu.VMEM((rows, head_dim), jnp.bfloat16),
            pltpu.VMEM((rows, head_dim), jnp.bfloat16),
            pltpu.VMEM((1, rows), jnp.int32),
            slots,
            pltpu.VMEM((blocks, 1, rows), jnp.float32),
            square,
            square,
            pltpu.VMEM((blocks, rows, rows), jnp.bfloat16),
            slots,
            slots,
            few,
            few,
            pltpu.SemaphoreType.DMA((5,)),
            sends,
            many,
            sends,
            many,
            sends,
            sends,
            sends,
            many,
            sends,
            sends,
        ],
        compiler_params=pltpu.CompilerParams(collective_id=0, has_side_effects=True),
    )(queries, keys, values, out_grads, positions.reshape(1, rows))
    return pl.pallas_call(
        put_out,
        out_shape=tuple(jax.ShapeDtypeStruct(one.shape, jnp.bfloat16) for one in results),
        in_specs=[near_space] * 3,
        out_specs=(any_space,) * 3,
        scratch_shapes=[pltpu.SemaphoreType.DMA((3,))],
    )(*(pltpu.with_memory_space_constraint(one, pltpu.VMEM) for one in held))


def solution(mesh):
    in_specs = (
        P("blk", ("team", "heads")),
        P(("blk", "team"), "heads"),
        P(("blk", "team"), "heads"),
        P("blk", ("team", "heads")),
        P("blk"),
    )
    out_specs = (
        P("blk", ("team", "heads")),
        P(("blk", "team"), "heads"),
        P(("blk", "team"), "heads"),
    )
    return jax.shard_map(
        per_device, mesh=mesh, in_specs=in_specs, out_specs=out_specs, check_vma=False
    )
```

time: 23.5 us -> 22.2 us (0.945)
  local copies, waits for them, and re-layouts: 2.68 us -> 0 us
  Pallas kernels: 19.7 us -> 21.3 us
    unnamed x7 -> x0, local copies, waits for them, and re-layouts: 2.68 us -> none
    pallas_call x1 -> x2, Pallas kernels: 19.7 us -> 21.3 us  [the longest x1 20.7 us: per_device(): pl.pallas_call(functools.partial(kernel, blocks, team), out_shape=tuple((...]
where the time goes in v2:
time: 22.2 us; the launch traced here: 22 us
  Pallas kernels  21.3 us (96%)
  between operations  0.64 us (3%)
    pallas_call x1, Pallas kernels, per_device(): pl.pallas_call(functools.partial(kernel, blocks, team), out_shape=tuple((...  20.7 us
    pallas_call x1, Pallas kernels, per_device(): pl.pallas_call(put_out, out_shape=tuple((jax.ShapeDtypeStruct(one.shape,...  0.65 us

profile of v2, /device:TPU:0, one launch (start us, length us, event | category | flops | bytes accessed | tf_op | source)
XLA Modules:
  0.0 22.0 jit_solution(5441085651501545904)
XLA Ops:
  0.6 20.7 %shard_map.76 = (bf16[128,128]{1,0:T(8,128)(2,1)S(1)}, bf16[32,128]{1,0:T(8,128)(2,1)S(1)}, bf16[32,128]{1,0:T(8,128)(2,1)S(1)}) custom-call(bf16[128,128]{1,0:T(8,128)(2,1)} %q_hbm.1, bf16[32,128]{1,0:T(8,128)(2,1)} %k_hbm.1, bf16[32,128]{1,0:T(8,128)(2,1)} %v_hbm.1, bf16[128,128]{1,0:T(8,128)(2,1)} %g_hbm.1, s32[1,128]{1,0:T(1,128)} %bitcast.1), custom_call_target="tpu_custom_call" | custom-call | tf_op jit(solution)/shard_map/pallas_call | solution.py:313
  21.3 0.6 %shard_map.77 = (bf16[128,128]{1,0:T(8,128)(2,1)}, bf16[32,128]{1,0:T(8,128)(2,1)}, bf16[32,128]{1,0:T(8,128)(2,1)}) custom-call(bf16[128,128]{1,0:T(8,128)(2,1)S(1)} %get-tuple-element.6.refs_0_, bf16[32,128]{1,0:T(8,128)(2,1)S(1)} %get-tuple-element.7.refs_1_, bf16[32,128]{1,0:T(8,128)(2,1)S(1)} %get-tuple-element.8.refs_2_), custom_call_target="tpu_custom_call" | custom-call | tf_op jit(solution)/shard_map/pallas_call | solution.py:345

commit v3 on v2

--- a/solution.py
+++ b/solution.py
@@ -69,6 +69,8 @@
     scores,
     products,
     slopes_ref,
+    columns,
+    tops,
     parts,
     staged,
     sums_ref,
@@ -116,6 +118,13 @@
     def wait_bytes(ref, sem):
         pltpu.make_async_copy(ref, ref, sem).wait()
 
+    barrier = pltpu.get_barrier_semaphore()
+
+    def greet(peer):
+        pl.semaphore_signal(barrier, inc=1, device_id=peer, device_id_type=MESH)
+
+    each(blocks - 1, lambda i: greet(blk_peer(block_at(blocks - 1 - i))))
+    each(team - 1, lambda i: greet(team_peer(mate_at(i + 1))))
     loads = [
         pltpu.make_async_copy(p_hbm, p_ref, load_sem.at[0]),
         pltpu.make_async_copy(k_hbm, kv.at[me, 0], load_sem.at[1]),
@@ -123,16 +132,9 @@
         pltpu.make_async_copy(q_hbm, q_ref, load_sem.at[3]),
         pltpu.make_async_copy(g_hbm, g_ref, load_sem.at[4]),
     ]
-    for load in loads:
-        load.start()
-
-    barrier = pltpu.get_barrier_semaphore()
-
-    def greet(peer):
-        pl.semaphore_signal(barrier, inc=1, device_id=peer, device_id_type=MESH)
-
-    each(blocks - 1, lambda i: greet(blk_peer(block_at(i + 1))))
-    each(team - 1, lambda i: greet(team_peer(mate_at(i + 1))))
+    for which in (1, 2, 0, 3, 4):
+        loads[which].start()
+
     loads[0].wait()
     place_row = p_ref[...].astype(jnp.float32)
     places[my_blk] = place_row
@@ -167,15 +169,25 @@
     def block_keys(blk_now, which):
         return join_rows(kv[pl.ds(blk_now * team, team), which])
 
-    def score_block(distance, top):
+    def make_columns(blk_now):
+        columns[blk_now] = jnp.transpose(jnp.broadcast_to(places[blk_now], (rows, rows)))
+
+    def score_block(distance, state):
+        top, total, trace = state
         blk_now = block_at(distance)
         wait_bytes(kv.at[pl.ds(0, team - 1)], pass_recv.at[blk_now])
-        columns = jnp.transpose(jnp.broadcast_to(places[blk_now], (rows, rows)))
         found = contract_last(block_keys(blk_now, 0), queries) * scale
-        masked = jnp.where(place_row >= columns, found, masked_score)
-        scores[blk_now] = masked
-        products[blk_now] = contract_last(block_keys(blk_now, 1), grads)
-        return jnp.maximum(top, jnp.max(masked, axis=0, keepdims=True))
+        block_products = contract_last(block_keys(blk_now, 1), grads)
+        masked = jnp.where(place_row >= columns[blk_now], found, masked_score)
+        updated = jnp.maximum(top, jnp.max(masked, axis=0, keepdims=True))
+        weights = jnp.exp(masked - updated)
+        scores[blk_now] = weights
+        products[blk_now] = block_products
+        tops[blk_now] = updated
+        factor = jnp.exp(top - updated)
+        total = total * factor + jnp.sum(weights, axis=0, keepdims=True)
+        trace = trace * factor + jnp.sum(weights * block_products, axis=0, keepdims=True)
+        return updated, total, trace
 
     def fold(body, init):
         if blocks <= 16:
@@ -188,36 +200,29 @@
     loads[4].wait()
     queries = q_ref[...]
     grads = g_ref[...]
-    top = jnp.full((1, rows), masked_score, jnp.float32)
+    nought = jnp.zeros((1, rows), jnp.float32)
+    state = (jnp.full((1, rows), masked_score, jnp.float32), nought, nought)
     if blocks <= 16:
         order = [near_first(index, blocks) for index in range(blocks)]
         for distance in order[1:]:
             pass_far(distance)
         wait_bytes(places.at[pl.ds(0, blocks - 1)], place_recv)
+        each(blocks, make_columns)
         for distance in order:
-            top = score_block(distance, top)
+            state = score_block(distance, state)
     else:
         order = None
         each(blocks - 1, lambda i: pass_far(i + 1))
         wait_bytes(places.at[pl.ds(0, blocks - 1)], place_recv)
-        top = fold(score_block, top)
-
-    def sums_of(blk_now, state):
-        total, trace = state
-        weights = jnp.exp(scores[blk_now] - top)
-        scores[blk_now] = weights
-        total = total + jnp.sum(weights, axis=0, keepdims=True)
-        trace = trace + jnp.sum(weights * products[blk_now], axis=0, keepdims=True)
-        return total, trace
-
-    nought = jnp.zeros((1, rows), jnp.float32)
-    total, trace = fold(sums_of, (nought, nought))
+        each(blocks, make_columns)
+        state = fold(score_block, state)
+    top, total, trace = state
     inverse = 1.0 / total
     delta = trace * inverse
 
     def grad_block(distance):
         blk_now = block_at(distance)
-        weights = scores[blk_now] * inverse
+        weights = scores[blk_now] * (inverse * jnp.exp(tops[blk_now] - top))
         rounded = weights.astype(jnp.bfloat16)
         slopes = (weights * (products[blk_now] - delta)).astype(jnp.bfloat16)
         slopes_ref[blk_now] = slopes
@@ -324,6 +329,8 @@
             square,
             square,
             pltpu.VMEM((blocks, rows, rows), jnp.bfloat16),
+            square,
+            pltpu.VMEM((blocks, 1, rows), jnp.float32),
             slots,
             slots,
             few,

time: 22.2 us -> 22.2 us (level)
  no operation moved by 1% of the time
where the time goes in v3:
time: 22.2 us; the launch traced here: 22 us
  Pallas kernels  21.3 us (96%)
  between operations  0.64 us (3%)
    pallas_call x1, Pallas kernels, per_device(): pl.pallas_call(functools.partial(kernel, blocks, team), out_shape=tuple((...  20.7 us
    pallas_call x1, Pallas kernels, per_device(): pl.pallas_call(put_out, out_shape=tuple((jax.ShapeDtypeStruct(one.shape,...  0.65 us

profile of v3, /device:TPU:0, one launch (start us, length us, event | category | flops | bytes accessed | tf_op | source)
XLA Modules:
  0.0 22.0 jit_solution(1544022037128246182)
XLA Ops:
  0.6 20.7 %shard_map.76 = (bf16[128,128]{1,0:T(8,128)(2,1)S(1)}, bf16[32,128]{1,0:T(8,128)(2,1)S(1)}, bf16[32,128]{1,0:T(8,128)(2,1)S(1)}) custom-call(bf16[128,128]{1,0:T(8,128)(2,1)} %q_hbm.1, bf16[32,128]{1,0:T(8,128)(2,1)} %k_hbm.1, bf16[32,128]{1,0:T(8,128)(2,1)} %v_hbm.1, bf16[128,128]{1,0:T(8,128)(2,1)} %g_hbm.1, s32[1,128]{1,0:T(1,128)} %bitcast.1), custom_call_target="tpu_custom_call" | custom-call | tf_op jit(solution)/shard_map/pallas_call | solution.py:318
  21.3 0.6 %shard_map.77 = (bf16[128,128]{1,0:T(8,128)(2,1)}, bf16[32,128]{1,0:T(8,128)(2,1)}, bf16[32,128]{1,0:T(8,128)(2,1)}) custom-call(bf16[128,128]{1,0:T(8,128)(2,1)S(1)} %get-tuple-element.6.refs_0_, bf16[32,128]{1,0:T(8,128)(2,1)S(1)} %get-tuple-element.7.refs_1_, bf16[32,128]{1,0:T(8,128)(2,1)S(1)} %get-tuple-element.8.refs_2_), custom_call_target="tpu_custom_call" | custom-call | tf_op jit(solution)/shard_map/pallas_call | solution.py:352
